TPU v7x, 32 devices: a whole 2x2x4 slice. The times are simulated.
32 devices in a mesh: row: 4 (over y, x), th: 4 (over z), ph: 2 (over core).
Axes of the slice: x: 2, y: 2, z: 4, core: 2. Of those that a mesh axis runs over, the one named last changes fastest.
Arguments:
- cells: float32 [8, 16, 64, 256], P(None, 'row', 'th', 'ph'), may hold values from -2 to 3, as said below
- faces: float32 [3, 16, 64, 256], P(None, 'row', 'th', 'ph'), may hold values from -3 to 3
Outputs:
- state: float32 [8, 16, 64, 256], P(None, 'row', 'th', 'ph')
- faces_new: float32 [3, 16, 64, 256], P(None, 'row', 'th', 'ph')
Inputs may be any that keep to these rules, and one draw needn't show every extreme that they name: `cells`: fields 0 and 4 (density, pressure) lie between 0.2 and 3; fields 1 to 3 between -0.5 and 0.5; fields 5 to 7 between -2 and 2.
All inputs are finite; a program needn't handle non-finite values.
Results may differ from a plain program's by a relative error of at most 0.0003.
Values sent between devices are 32-bit elements; how exact they have to be, the bound alone decides.
A program may use at most 64 MiB of HBM per device.

v0:
```python
import jax
import jax.numpy as jnp
from jax import lax
from jax.sharding import PartitionSpec as P

adiabatic = 5.0 / 3.0
step_size = 0.05


def padded_2(cells, sides, width):
    for axis, dim in sides:
        count = lax.axis_size(axis)
        head = lax.slice_in_dim(cells, 0, width, axis=dim)
        tail = lax.slice_in_dim(cells, cells.shape[dim] - width, cells.shape[dim], axis=dim)
        cells = jnp.concatenate(
            [
                lax.ppermute(tail, axis, [(i, (i + 1) % count) for i in range(count)]),
                cells,
                lax.ppermute(head, axis, [((i + 1) % count, i) for i in range(count)]),
            ],
            axis=dim,
        )
    return cells


def conserved_flux(padded):
    density = padded[0]
    velocity = padded[1:4]
    pressure = padded[4]
    magnetic = padded[5:8]
    kinetic = 0.5 * density * jnp.sum(velocity * velocity, axis=0)
    magnetic_sq = jnp.sum(magnetic * magnetic, axis=0)
    energy = pressure / (adiabatic - 1.0) + kinetic + 0.5 * magnetic_sq
    total_press = pressure + 0.5 * magnetic_sq
    alignment = jnp.sum(velocity * magnetic, axis=0)
    fast_speed = jnp.sqrt((adiabatic * pressure + magnetic_sq) / density)
    conserved = jnp.stack(
        [density, density * velocity[0], density * velocity[1], density * velocity[2], energy]
    )
    fluxes = []
    speeds = []
    for direction in range(3):
        moving = velocity[direction]
        normal_field = magnetic[direction]
        entries = [density * moving]
        for component in range(3):
            moment = density * velocity[component] * moving - magnetic[component] * normal_field
            if component == direction:
                moment = moment + total_press
            entries.append(moment)
        entries.append((energy + total_press) * moving - normal_field * alignment)
        fluxes.append(jnp.stack(entries))
        speeds.append(jnp.abs(moving) + fast_speed)
    return (conserved, fluxes, speeds)


def hydro_change(padded):
    conserved, fluxes, speeds = conserved_flux(padded)
    change = jnp.zeros_like(conserved[:, 1:-1, 1:-1, 1:-1])
    for direction in range(3):
        keeper = [slice(None), slice(1, -1), slice(1, -1), slice(1, -1)]
        keeper[direction + 1] = slice(None)
        lower_cut = [slice(None)] * 4
        upper_cut = [slice(None)] * 4
        lower_cut[direction + 1] = slice(0, -1)
        upper_cut[direction + 1] = slice(1, None)
        state_cut = conserved[tuple(keeper)]
        flux_cut = fluxes[direction][tuple(keeper)]
        speed_cut = speeds[direction][tuple(keeper[1:])]
        wave_speed = jnp.maximum(speed_cut[tuple(lower_cut[1:])], speed_cut[tuple(upper_cut[1:])])
        face_flux = 0.5 * (
            flux_cut[tuple(lower_cut)] + flux_cut[tuple(upper_cut)]
        ) - 0.5 * wave_speed * (state_cut[tuple(upper_cut)] - state_cut[tuple(lower_cut)])
        change = change + face_flux[tuple(upper_cut)] - face_flux[tuple(lower_cut)]
    return conserved[:, 1:-1, 1:-1, 1:-1] - step_size * change


def edge_fields(padded):
    velocity = padded[1:4]
    magnetic = padded[5:8]
    emf_first = -(velocity[1] * magnetic[2] - velocity[2] * magnetic[1])
    emf_second = -(velocity[2] * magnetic[0] - velocity[0] * magnetic[2])
    emf_third = -(velocity[0] * magnetic[1] - velocity[1] * magnetic[0])
    inner = emf_first[1:-1]
    edge_one = 0.25 * (
        inner[:, :-1, :-1] + inner[:, 1:, :-1] + inner[:, :-1, 1:] + inner[:, 1:, 1:]
    )
    inner = emf_second[:, 1:-1, :]
    edge_two = 0.25 * (
        inner[:-1, :, :-1] + inner[1:, :, :-1] + inner[:-1, :, 1:] + inner[1:, :, 1:]
    )
    inner = emf_third[:, :, 1:-1]
    edge_three = 0.25 * (inner[:-1, :-1] + inner[1:, :-1] + inner[:-1, 1:] + inner[1:, 1:])
    return (edge_one, edge_two, edge_three)


def face_advance(first, second, third, edge_one, edge_two, edge_three):
    new_first = first - step_size * (
        edge_three[:, 1:] - edge_three[:, :-1] - (edge_two[:, :, 1:] - edge_two[:, :, :-1])
    )
    new_second = second - step_size * (
        edge_one[:, :, 1:] - edge_one[:, :, :-1] - (edge_three[1:] - edge_three[:-1])
    )
    new_third = third - step_size * (
        edge_two[1:] - edge_two[:-1] - (edge_one[:, 1:] - edge_one[:, :-1])
    )
    return (new_first, new_second, new_third)


def fix_radial(padded, at_bottom, at_top):
    lowest = jnp.where(at_bottom, padded[:, 1:2], padded[:, :1])
    highest = jnp.where(at_top, padded[:, -2:-1], padded[:, -1:])
    return jnp.concatenate([lowest, padded[:, 1:-1], highest], axis=1)


def fix_polar(padded, at_north, at_south):
    field_ids = jnp.arange(padded.shape[0])
    flipper = (
        jnp.where((field_ids == 2) | (field_ids == 7), -1.0, 1.0)
        .astype(jnp.float32)
        .reshape(-1, 1, 1, 1)
    )
    lowest = jnp.where(at_north, padded[:, :, 1:2] * flipper, padded[:, :, :1])
    highest = jnp.where(at_south, padded[:, :, -2:-1] * flipper, padded[:, :, -1:])
    return jnp.concatenate([lowest, padded[:, :, 1:-1], highest], axis=2)


def on_device(cells, faces):
    row_place = lax.axis_index("row")
    polar_place = lax.axis_index("th")
    at_bottom = row_place == 0
    at_top = row_place == lax.axis_size("row") - 1
    at_north = polar_place == 0
    at_south = polar_place == lax.axis_size("th") - 1
    source = jnp.concatenate([cells, faces], axis=0)
    padded = padded_2(source, (("row", 1), ("th", 2), ("ph", 3)), 1)
    padded = fix_radial(padded, at_bottom, at_top)
    padded = fix_polar(padded, at_north, at_south)
    cell_part = padded[:8]
    conserved_new = hydro_change(cell_part)
    edge_one, edge_two, edge_three = edge_fields(cell_part)
    radial_cells = faces.shape[1]
    polar_cells = faces.shape[2]
    first_ext = jnp.concatenate([faces[0], padded[8, -1:, 1:-1, 1:-1]], axis=0)
    second_ext = jnp.concatenate([faces[1], padded[9, 1:-1, -1:, 1:-1]], axis=1)
    third_ext = jnp.concatenate([faces[2], padded[10, 1:-1, 1:-1, -1:]], axis=2)
    new_first, new_second, new_third = face_advance(
        first_ext, second_ext, third_ext, edge_one, edge_two, edge_three
    )
    upper_first = jnp.concatenate(
        [new_first[1:-1], jnp.where(at_top, new_first[-2:-1], new_first[-1:])], axis=0
    )
    upper_second = jnp.concatenate(
        [new_second[:, 1:-1], jnp.where(at_south, 0.0, new_second[:, -1:])], axis=1
    )
    upper_third = new_third[:, :, 1:]
    new_first = new_first[:radial_cells]
    new_second = new_second[:, :polar_cells]
    new_third = new_third[:, :, :-1]
    centred = 0.5 * jnp.stack(
        [new_first + upper_first, new_second + upper_second, new_third + upper_third]
    )
    state = jnp.concatenate([conserved_new, centred], axis=0)
    return (state, jnp.stack([new_first, new_second, new_third]))


def solution(mesh):
    return jax.shard_map(
        on_device,
        mesh=mesh,
        in_specs=(P(None, "row", "th", "ph"), P(None, "row", "th", "ph")),
        out_specs=(P(None, "row", "th", "ph"), P(None, "row", "th", "ph")),
        check_vma=False,
    )
```

profile of v0, /device:TPU:0, one launch (start us, length us, event | category | flops | bytes accessed | tf_op | source)
XLA Modules:
  0.0 29.9 jit_solution(7105299752882524390)
XLA Ops:
  0.6 1.0 %constant_dynamic-update-slice_fusion.1 = f32[11,4,16,128]{3,2,1,0:T(8,128)S(1)} fusion(f32[8,4,16,128]{3,2,1,0:T(8,128)} %param.2), kind=kLoop, calls=%fused_computation.104 | loop fusion | bytes 524288
  1.6 0.9 %constant_dynamic-update-slice_fusion = f32[11,4,16,128]{3,2,1,0:T(8,128)S(1)} fusion(f32[11,4,16,128]{3,2,1,0:T(8,128)S(1)} %constant_dynamic-update-slice_fusion.1, f32[3,4,16,128]{3,2,1,0:T(8,128)} %param.3), kind=kLoop, calls=%fused_computation.103 | loop fusion | bytes 196608 | tf_op jit(solution)/shard_map/concatenate | solution.py:135
  2.6 3.0 %collective-permute-start = (f32[11,1,16,128]{3,2,1,0:T(8,128)S(1)}, f32[11,1,16,128]{3,2,1,0:T(8,128)S(1)}, u32[]{:S(2)}, u32[]{:S(2)}) collective-permute-start(f32[11,1,16,128]{3,2,1,0:T(8,128)S(1)} %get-tuple-element.44), channel_id=1, source_target_pairs={{0,8},{8,16},{16,24},{24,0},{1,9},{9,17},{17,25},{25,1},{2,10},{10... | collective-permute-start | bytes 270344 | tf_op jit(solution)/shard_map/ppermute | solution.py:17
  5.6 1.0 %collective-permute-start.1 = (f32[11,1,16,128]{3,2,1,0:T(8,128)S(1)}, f32[11,1,16,128]{3,2,1,0:T(8,128)S(1)}, u32[]{:S(2)}, u32[]{:S(2)}) collective-permute-start(f32[11,1,16,128]{3,2,1,0:T(8,128)S(1)} %get-tuple-element.45), channel_id=1, source_target_pairs={{8,0},{16,8},{24,16},{0,24},{9,1},{17,9},{25,17},{1,25},{10,2},{18... | collective-permute-start | bytes 270344 | tf_op jit(solution)/shard_map/ppermute | solution.py:19
  6.6 3.0 %collective-permute-done = f32[11,1,16,128]{3,2,1,0:T(8,128)S(1)} collective-permute-done((f32[11,1,16,128]{3,2,1,0:T(8,128)S(1)}, f32[11,1,16,128]{3,2,1,0:T(8,128)S(1)}, u32[]{:S(2)}, u32[]{:S(2)}) %collective-permute-start) | collective-permute-done | bytes 90144 | tf_op jit(solution)/shard_map/ppermute | solution.py:17
  9.6 1.7 %collective-permute-done.1 = f32[11,1,16,128]{3,2,1,0:T(8,128)S(1)} collective-permute-done((f32[11,1,16,128]{3,2,1,0:T(8,128)S(1)}, f32[11,1,16,128]{3,2,1,0:T(8,128)S(1)}, u32[]{:S(2)}, u32[]{:S(2)}) %collective-permute-start.1) | collective-permute-done | bytes 90144 | tf_op jit(solution)/shard_map/ppermute | solution.py:19
  11.4 1.6 %collective-permute-start.2 = (f32[11,6,1,128]{3,2,1,0:T(1,128)S(1)}, f32[11,6,1,128]{3,2,1,0:T(1,128)S(1)}, u32[]{:S(2)}, u32[]{:S(2)}) collective-permute-start(f32[11,6,1,128]{3,2,1,0:T(1,128)S(1)} %get-tuple-element.33), channel_id=1, source_target_pairs={{0,2},{2,4},{4,6},{6,0},{1,3},{3,5},{5,7},{7,1},{8,10},{10,12},{12... | collective-permute-start | bytes 101384 | tf_op jit(solution)/shard_map/ppermute | solution.py:17
  13.0 2.2 %collective-permute-start.3 = (f32[11,6,1,128]{3,2,1,0:T(1,128)S(1)}, f32[11,6,1,128]{3,2,1,0:T(1,128)S(1)}, u32[]{:S(2)}, u32[]{:S(2)}) collective-permute-start(f32[11,6,1,128]{3,2,1,0:T(1,128)S(1)} %get-tuple-element.34), channel_id=1, source_target_pairs={{2,0},{4,2},{6,4},{0,6},{3,1},{5,3},{7,5},{1,7},{10,8},{12,10},{14... | collective-permute-start | bytes 101384 | tf_op jit(solution)/shard_map/ppermute | solution.py:19
  15.3 2.0 %collective-permute-done.2 = f32[11,6,1,128]{3,2,1,0:T(1,128)S(1)} collective-permute-done((f32[11,6,1,128]{3,2,1,0:T(1,128)S(1)}, f32[11,6,1,128]{3,2,1,0:T(1,128)S(1)}, u32[]{:S(2)}, u32[]{:S(2)}) %collective-permute-start.2) | collective-permute-done | bytes 33824 | tf_op jit(solution)/shard_map/ppermute | solution.py:17
  17.7 0.5 %copy.33 = f32[11,6,18,1]{2,3,1,0:T(1,128)S(1)} copy(f32[11,6,18,1]{3,2,1,0:T(8,128)S(1)} %get-tuple-element.31) | data formatting | bytes 9504
  18.2 0.5 %copy.34 = f32[11,6,18,1]{2,3,1,0:T(1,128)S(1)} copy(f32[11,6,18,1]{3,2,1,0:T(8,128)S(1)} %get-tuple-element.32) | data formatting | bytes 9504
  18.8 0.5 %collective-permute-start.4 = (f32[11,6,18,1]{2,3,1,0:T(1,128)S(1)}, f32[11,6,18,1]{2,3,1,0:T(1,128)S(1)}, u32[]{:S(2)}, u32[]{:S(2)}) collective-permute-start(f32[11,6,18,1]{2,3,1,0:T(1,128)S(1)} %copy.33), channel_id=1, source_target_pairs={{0,1},{1,0},{2,3},{3,2},{4,5},{5,4},{6,7},{7,6},{8,9},{9,8},{10,11... | collective-permute-start | bytes 14264 | tf_op jit(solution)/shard_map/ppermute | solution.py:17
  19.3 0.8 %collective-permute-done.4 = f32[11,6,18,1]{2,3,1,0:T(1,128)S(1)} collective-permute-done((f32[11,6,18,1]{2,3,1,0:T(1,128)S(1)}, f32[11,6,18,1]{2,3,1,0:T(1,128)S(1)}, u32[]{:S(2)}, u32[]{:S(2)}) %collective-permute-start.4) | collective-permute-done | bytes 4784 | tf_op jit(solution)/shard_map/ppermute | solution.py:17
  20.1 0.5 %copy.28 = f32[11,6,18,1]{3,2,1,0:T(8,128)S(1)} copy(f32[11,6,18,1]{2,3,1,0:T(1,128)S(1)} %collective-permute-done.4) | data formatting | bytes 9504 | tf_op jit(solution)/shard_map/ppermute | solution.py:17
  20.7 0.5 %copy.29 = f32[11,6,18,1]{3,2,1,0:T(8,128)S(1)} copy(f32[11,6,18,1]{2,3,1,0:T(1,128)S(1)} %collective-permute-done.5) | data formatting | bytes 9504 | tf_op jit(solution)/shard_map/ppermute | solution.py:19
  21.2 1.0 %pad_maximum_fusion = f32[11,6,18,130]{3,2,1,0:T(8,128)S(1)} fusion(f32[11,6,18,1]{3,2,1,0:T(8,128)S(1)} %copy.29, f32[11,6,1,128]{3,2,1,0:T(1,128)S(1)} %collective-permute-done.3, f32[11,1,16,128]{3,2,1,0:T(8,128)S(1)} %collective-permute-done.1, f32[11,4,16,128]{3,2,1,0:T(8,128)S(1)} %constant_dynamic-update-slice_fusion, ...), kind=kLoop, calls=%fused_computation | loop fusion | flops 926640 | bytes 1235520 | tf_op jit(solution)/shard_map/concatenate | solution.py:15
  22.3 0.4 %maximum_select_fusion = f32[11,1,18,130]{3,2,1,0:T(8,128)S(1)} fusion(f32[11,6,18,1]{3,2,1,0:T(8,128)S(1)} %copy.29, f32[11,6,18,1]{3,2,1,0:T(8,128)S(1)} %copy.28, f32[11,6,1,128]{3,2,1,0:T(1,128)S(1)} %collective-permute-done.3, f32[11,6,1,128]{3,2,1,0:T(1,128)S(1)} %collective-permute-done.2, f32[11,1,16,128]{3,2,1,0:T(8,128)S(1)} %collective-permute-done.1, ...), kind=kLoop, calls=%fused_computation.12 | loop fusion | flops 334620 | bytes 720721 | tf_op jit(solution)/shard_map/jit(_where)/select_n | solution.py:112
  22.7 0.4 %maximum_select_fusion.1 = f32[11,1,18,130]{3,2,1,0:T(8,128)S(1)} fusion(f32[11,6,18,1]{3,2,1,0:T(8,128)S(1)} %copy.29, f32[11,6,18,1]{3,2,1,0:T(8,128)S(1)} %copy.28, f32[11,6,1,128]{3,2,1,0:T(1,128)S(1)} %collective-permute-done.3, f32[11,6,1,128]{3,2,1,0:T(1,128)S(1)} %collective-permute-done.2, f32[11,1,16,128]{3,2,1,0:T(8,128)S(1)} %collective-permute-done.1, ...), kind=kLoop, calls=%fused_computation.13 | loop fusion | flops 334620 | bytes 720721 | tf_op jit(solution)/shard_map/jit(_where)/select_n | solution.py:111
  23.8 0.3 %pad_maximum_fusion.2 = f32[11,6,18,130]{3,2,1,0:T(8,128)S(1)} fusion(f32[11,6,1,130]{3,2,1,0:T(1,128)S(1)} %get-tuple-element.30, f32[11,6,16,130]{3,2,1,0:T(8,128)S(1)} %slice.459, f32[11,6,1,130]{3,2,1,0:T(1,128)S(1)} %get-tuple-element.29), kind=kLoop, calls=%fused_computation.2 | loop fusion | flops 308880 | bytes 1235520 | tf_op jit(solution)/shard_map/concatenate | solution.py:125
  25.3 0.4 %copy-done = f32[5,6,18,130]{3,2,1,0:T(8,128)} copy-done((f32[5,6,18,130]{3,2,1,0:T(8,128)}, f32[5,6,18,130]{3,2,1,0:T(8,128)S(1)}, u32[]{:S(2)}) %copy-start) | copy-done | bytes 280824
  26.8 0.7 %copy-done.1 = f32[5,6,18,130]{3,2,1,0:T(8,128)S(1)} copy-done((f32[5,6,18,130]{3,2,1,0:T(8,128)S(1)}, f32[5,6,18,130]{3,2,1,0:T(8,128)}, u32[]{:S(2)}) %copy-start.1) | copy-done | bytes 280824
  27.7 0.3 %fusion.4 = f32[5,4,17,128]{3,2,1,0:T(8,128)S(1)} fusion(f32[5,6,18,130]{3,2,1,0:T(8,128)S(1)} %get-tuple-element.54, f32[5,6,18,130]{3,2,1,0:T(8,128)S(1)} %get-tuple-element.35, f32[4,17,128]{2,1,0:T(8,128)S(1)} %fusion.29), kind=kLoop, calls=%fused_computation.17 | loop fusion | flops 217600 | bytes 905216 | tf_op jit(solution)/shard_map/sub | solution.py:71
  28.5 0.7 %pad_maximum_fusion.4 = f32[8,4,16,128]{3,2,1,0:T(8,128)} fusion(f32[3,4,16,128]{3,2,1,0:T(8,128)S(1)} %maximum_multiply_fusion, f32[5,4,16,128]{3,2,1,0:T(8,128)S(1)} %fusion.10), kind=kLoop, calls=%fused_computation.14 | loop fusion | flops 65536 | bytes 524288 | tf_op jit(solution)/shard_map/concatenate | solution.py:163
  29.3 0.6 %pad_maximum_fusion.13 = f32[3,4,16,128]{3,2,1,0:T(8,128)} fusion(f32[1,4,16,128]{3,2,1,0:T(8,128)S(1)} %get-tuple-element.60, f32[1,4,16,128]{3,2,1,0:T(8,128)S(1)} %get-tuple-element.62, f32[1,4,16,128]{3,2,1,0:T(8,128)S(1)} %get-tuple-element.64), kind=kLoop, calls=%fused_computation.78 | loop fusion | flops 49152 | bytes 196608 | tf_op jit(solution)/shard_map/stack | solution.py:164
  (62 shorter events, 4.3 us)
Async XLA Ops:
  0.6 14.6 %copy-start.2 = (f32[3,4,16,128]{3,2,1,0:T(8,128)S(1)}, f32[3,4,16,128]{3,2,1,0:T(8,128)}, u32[]{:S(2)}) copy-start(f32[3,4,16,128]{3,2,1,0:T(8,128)} %param.3) | copy-start | bytes 294916
  2.6 7.1 %collective-permute-start = (f32[11,1,16,128]{3,2,1,0:T(8,128)S(1)}, f32[11,1,16,128]{3,2,1,0:T(8,128)S(1)}, u32[]{:S(2)}, u32[]{:S(2)}) collective-permute-start(f32[11,1,16,128]{3,2,1,0:T(8,128)S(1)} %get-tuple-element.44), channel_id=1, source_target_pairs={{0,8},{8,16},{16,24},{24,0},{1,9},{9,17},{17,25},{25,1},{2,10},{10... | collective-permute-start | bytes 270344 | tf_op jit(solution)/shard_map/ppermute | solution.py:17
  5.6 5.8 %collective-permute-start.1 = (f32[11,1,16,128]{3,2,1,0:T(8,128)S(1)}, f32[11,1,16,128]{3,2,1,0:T(8,128)S(1)}, u32[]{:S(2)}, u32[]{:S(2)}) collective-permute-start(f32[11,1,16,128]{3,2,1,0:T(8,128)S(1)} %get-tuple-element.45), channel_id=1, source_target_pairs={{8,0},{16,8},{24,16},{0,24},{9,1},{17,9},{25,17},{1,25},{10,2},{18... | collective-permute-start | bytes 270344 | tf_op jit(solution)/shard_map/ppermute | solution.py:19
  11.4 5.9 %collective-permute-start.2 = (f32[11,6,1,128]{3,2,1,0:T(1,128)S(1)}, f32[11,6,1,128]{3,2,1,0:T(1,128)S(1)}, u32[]{:S(2)}, u32[]{:S(2)}) collective-permute-start(f32[11,6,1,128]{3,2,1,0:T(1,128)S(1)} %get-tuple-element.33), channel_id=1, source_target_pairs={{0,2},{2,4},{4,6},{6,0},{1,3},{3,5},{5,7},{7,1},{8,10},{10,12},{12... | collective-permute-start | bytes 101384 | tf_op jit(solution)/shard_map/ppermute | solution.py:17
  13.0 4.3 %collective-permute-start.3 = (f32[11,6,1,128]{3,2,1,0:T(1,128)S(1)}, f32[11,6,1,128]{3,2,1,0:T(1,128)S(1)}, u32[]{:S(2)}, u32[]{:S(2)}) collective-permute-start(f32[11,6,1,128]{3,2,1,0:T(1,128)S(1)} %get-tuple-element.34), channel_id=1, source_target_pairs={{2,0},{4,2},{6,4},{0,6},{3,1},{5,3},{7,5},{1,7},{10,8},{12,10},{14... | collective-permute-start | bytes 101384 | tf_op jit(solution)/shard_map/ppermute | solution.py:19
  18.7 1.9 %collective-permute-start.5 = (f32[11,6,18,1]{2,3,1,0:T(1,128)S(1)}, f32[11,6,18,1]{2,3,1,0:T(1,128)S(1)}, u32[]{:S(2)}, u32[]{:S(2)}) collective-permute-start(f32[11,6,18,1]{2,3,1,0:T(1,128)S(1)} %copy.34), channel_id=1, source_target_pairs={{1,0},{0,1},{3,2},{2,3},{5,4},{4,5},{7,6},{6,7},{9,8},{8,9},{11,10... | collective-permute-start | bytes 14264 | tf_op jit(solution)/shard_map/ppermute | solution.py:19
  18.8 1.4 %collective-permute-start.4 = (f32[11,6,18,1]{2,3,1,0:T(1,128)S(1)}, f32[11,6,18,1]{2,3,1,0:T(1,128)S(1)}, u32[]{:S(2)}, u32[]{:S(2)}) collective-permute-start(f32[11,6,18,1]{2,3,1,0:T(1,128)S(1)} %copy.33), channel_id=1, source_target_pairs={{0,1},{1,0},{2,3},{3,2},{4,5},{5,4},{6,7},{7,6},{8,9},{9,8},{10,11... | collective-permute-start | bytes 14264 | tf_op jit(solution)/shard_map/ppermute | solution.py:17
  24.8 0.9 %copy-start = (f32[5,6,18,130]{3,2,1,0:T(8,128)}, f32[5,6,18,130]{3,2,1,0:T(8,128)S(1)}, u32[]{:S(2)}) copy-start(f32[5,6,18,130]{3,2,1,0:T(8,128)S(1)} %get-tuple-element.46) | copy-start | bytes 842404
  25.2 0.6 %copy-start.3 = (f32[5,16,128]{2,1,0:T(8,128)}, f32[5,16,128]{2,1,0:T(8,128)S(1)}, u32[]{:S(2)}) copy-start(f32[5,16,128]{2,1,0:T(8,128)S(1)} %fusion.32) | copy-start | bytes 122884
  25.9 0.9 %copy-start.4 = (f32[5,16,128]{2,1,0:T(8,128)S(1)}, f32[5,16,128]{2,1,0:T(8,128)}, u32[]{:S(2)}) copy-start(f32[5,16,128]{2,1,0:T(8,128)} %copy-done.3) | copy-start | bytes 122884
  25.9 0.9 %slice-start = ((f32[5,16,128]{2,1,0:T(8,128)}), f32[3,16,128]{2,1,0:T(8,128)S(1)}, s32[]{:S(2)}) async-start(f32[5,16,128]{2,1,0:T(8,128)} %copy-done.3), calls=%async_computation | async-start | bytes 49152 | tf_op jit(solution)/shard_map/slice | solution.py:151
  26.3 1.1 %copy-start.1 = (f32[5,6,18,130]{3,2,1,0:T(8,128)S(1)}, f32[5,6,18,130]{3,2,1,0:T(8,128)}, u32[]{:S(2)}) copy-start(f32[5,6,18,130]{3,2,1,0:T(8,128)} %copy-done) | copy-start | bytes 842404
where the time goes:
time: 30.1 us; the launch traced here: 29.9 us
  starting transfers between devices  8.47 us (28%)
  waiting for transfers between devices  7.6 us (25%)
  other arithmetic  6.92 us (23%)
  local copies, waits for them, and re-layouts  5.95 us (20%)
  between operations  0.97 us (3%)
    ppermute x3, waiting for transfers between devices, padded_2(): lax.ppermute(tail, axis, [(i, (i + 1) % count) for i in range(count)])  5.85 us
    ppermute x3, starting transfers between devices, padded_2(): lax.ppermute(tail, axis, [(i, (i + 1) % count) for i in range(count)])  5.14 us
    ppermute x3, starting transfers between devices, padded_2(): lax.ppermute(head, axis, [((i + 1) % count, i) for i in range(count)])  3.32 us
    unnamed x16, local copies, waits for them, and re-layouts  3.12 us
    ppermute x3, waiting for transfers between devices, padded_2(): lax.ppermute(head, axis, [((i + 1) % count, i) for i in range(count)])  1.75 us
    concatenate x2, other arithmetic, padded_2(): jnp.concatenate([lax.ppermute(tail, axis, [(i, (i + 1) % count) for i in...  1.11 us
    concatenate x1, local copies, waits for them, and re-layouts, on_device(): source = jnp.concatenate([cells, faces], axis=0)  0.9 us
    sub x3, other arithmetic, hydro_change(): 0.5 * (flux_cut[tuple(lower_cut)] + flux_cut[tuple(upper_cut)])  0.86 us
  transfers between devices with their start and end apart: 6, of which 4 were waited for; matrix products, arithmetic and copies ran while one was open for 2% of the time, Pallas kernels for 0%

commit v1 on v0

v1 whole, which is shorter than its diff:
```python
import functools

import jax
import jax.numpy as jnp
from jax import lax
from jax.experimental import pallas as pl
from jax.experimental.pallas import tpu as pltpu
from jax.sharding import PartitionSpec as P

adiabatic = 5.0 / 3.0
step_size = 0.05
MESH = pl.DeviceIdType.MESH


def derived(prim, direction):
    density, velocity, pressure, magnetic = prim[0], prim[1:4], prim[4], prim[5:8]
    kinetic = 0.5 * density * (
        velocity[0] * velocity[0] + velocity[1] * velocity[1] + velocity[2] * velocity[2]
    )
    magnetic_sq = (
        magnetic[0] * magnetic[0] + magnetic[1] * magnetic[1] + magnetic[2] * magnetic[2]
    )
    energy = pressure / (adiabatic - 1.0) + kinetic + 0.5 * magnetic_sq
    total_press = pressure + 0.5 * magnetic_sq
    alignment = (
        velocity[0] * magnetic[0] + velocity[1] * magnetic[1] + velocity[2] * magnetic[2]
    )
    fast_speed = jnp.sqrt((adiabatic * pressure + magnetic_sq) / density)
    conserved = [density] + [density * v for v in velocity] + [energy]
    moving, normal_field = velocity[direction], magnetic[direction]
    flux = [conserved[1 + direction]]
    for component in range(3):
        moment = conserved[1 + component] * moving - magnetic[component] * normal_field
        if component == direction:
            moment = moment + total_press
        flux.append(moment)
    flux.append((energy + total_press) * moving - normal_field * alignment)
    return conserved, flux, jnp.abs(moving) + fast_speed


def face_flux(low, high):
    wave = 0.5 * jnp.maximum(low[2], high[2])
    return [
        0.5 * (low[1][i] + high[1][i]) - wave * (high[0][i] - low[0][i]) for i in range(5)
    ]


def emf_first(p):
    return p[3] * p[6] - p[2] * p[7]


def emf_second(p):
    return p[1] * p[7] - p[3] * p[5]


def emf_third(p):
    return p[2] * p[5] - p[1] * p[6]


def kernel(
    sizes,
    cells_hbm,
    faces_hbm,
    state,
    faces_new,
    cells,
    faces,
    from_ph,
    face_ph,
    pack_own,
    pack_ph,
    pack_row,
    from_th,
    face_th,
    from_thph,
    from_row,
    face_row,
    from_rowth,
    local_sem,
    send_sem,
    recv_sem,
):
    n_row, n_th, n_ph = sizes
    R, T, L = cells.shape[1:]
    half = L // 2
    row, th, ph = lax.axis_index("row"), lax.axis_index("th"), lax.axis_index("ph")
    at_bottom, at_top = row == 0, row == n_row - 1
    at_north, at_south = th == 0, th == n_th - 1
    left = lax.rem(ph + n_ph - 1, n_ph)
    right = lax.rem(ph + 1, n_ph)
    below, above = {"row": row - 1}, {"row": row + 1}
    north, south = {"th": th - 1}, {"th": th + 1}
    ph_targets = [{"ph": left}] if n_ph == 2 else [{"ph": left}, {"ph": right}]
    slots = len(ph_targets)

    barrier = pltpu.get_barrier_semaphore()
    greet = [
        (jnp.logical_not(at_bottom), below),
        (jnp.logical_not(at_top), above),
        (jnp.logical_not(at_north), north),
        (jnp.logical_not(at_south), south),
    ]
    for exists, who in greet:
        @pl.when(exists)
        def _():
            pl.semaphore_signal(barrier, inc=1, device_id=who, device_id_type=MESH)
    for who in ph_targets:
        pl.semaphore_signal(barrier, inc=1, device_id=who, device_id_type=MESH)

    load_cells = pltpu.make_async_copy(cells_hbm, cells, local_sem.at[0])
    load_faces = pltpu.make_async_copy(faces_hbm, faces, local_sem.at[1])
    load_cells.start()
    load_faces.start()

    count = [0]
    transfers = []

    def transfer(src, dst, who, sends=None, receives=None):
        index = count[0]
        count[0] += 1
        copy = pltpu.make_async_remote_copy(
            src_ref=src,
            dst_ref=dst,
            send_sem=send_sem.at[index],
            recv_sem=recv_sem.at[index],
            device_id=who,
            device_id_type=MESH,
        )

        def guarded(condition, action):
            if condition is None:
                action()
            else:
                pl.when(condition)(lambda: action())

        entry = (
            lambda: guarded(sends, copy.start),
            lambda: guarded(receives, copy.wait_recv),
            lambda: guarded(sends, copy.wait_send),
        )
        transfers.append(entry)
        return entry

    not_bottom, not_top, not_north, not_south = [g[0] for g in greet]
    first_row, last_row = pl.ds(0, 1), pl.ds(T - 1, 1)
    row_up = transfer(cells.at[:, R - 1], from_row.at[0], above, not_top, not_bottom)
    row_down = transfer(cells.at[:, 0], from_row.at[1], below, not_bottom, not_top)
    row_face = transfer(faces.at[0, 0], face_row, below, not_bottom, not_top)
    th_up = transfer(cells.at[:, :, last_row], from_th.at[0], south, not_south, not_north)
    th_down = transfer(cells.at[:, :, first_row], from_th.at[1], north, not_north, not_south)
    th_face = transfer(faces.at[1, :, first_row], face_th, north, not_north, not_south)
    ph_cells = [transfer(cells, from_ph.at[s], ph_targets[s]) for s in range(slots)]
    ph_pack = [transfer(pack_own, pack_ph.at[s], ph_targets[s]) for s in range(slots)]
    ph_face = transfer(faces.at[2], face_ph, ph_targets[0])
    corner = []
    for s in range(slots):
        corner.append(
            transfer(
                from_ph.at[s, pl.ds(2, 6), :, last_row], from_thph.at[s, 0], south, not_south, not_north
            )
        )
        corner.append(
            transfer(
                from_ph.at[s, pl.ds(2, 6), :, first_row], from_thph.at[s, 1], north, not_north, not_south
            )
        )
    packs = []
    for s in range(slots):
        packs.append(
            transfer(pack_ph.at[s, 1], pack_row.at[s, 0], above, not_top, not_bottom)
        )
        packs.append(
            transfer(pack_ph.at[s, 0], pack_row.at[s, 1], below, not_bottom, not_top)
        )
    rowth = []
    for side, has in ((0, not_north), (1, not_south)):
        rowth.append(
            transfer(
                from_th.at[side, pl.ds(1, 6), R - 1],
                from_rowth.at[0, side],
                above,
                jnp.logical_and(not_top, has),
                jnp.logical_and(not_bottom, has),
            )
        )
        rowth.append(
            transfer(
                from_th.at[side, pl.ds(1, 6), 0],
                from_rowth.at[1, side],
                below,
                jnp.logical_and(not_bottom, has),
                jnp.logical_and(not_top, has),
            )
        )

    lane = lax.broadcasted_iota(jnp.int32, (T, L), 1)
    sub = lax.broadcasted_iota(jnp.int32, (T, L), 0)

    load_cells.wait()
    for where, layer in ((0, 0), (1, R - 1)):
        e = emf_second([cells[f, layer] for f in range(8)])
        first_column = jnp.broadcast_to(e[:, :1], (T, L))
        last_column = jnp.broadcast_to(e[:, L - 1 :], (T, L))
        spread = jnp.where(lane == sub, first_column, 0.0) + jnp.where(
            lane == sub + half, last_column, 0.0
        )
        pack_own[where] = jnp.sum(spread, axis=0, keepdims=True)
    load_faces.wait()

    peers = slots + sum(exists.astype(jnp.int32) for exists, _ in greet)
    pl.semaphore_wait(barrier, peers)

    odd = lax.rem(row, 2) == 1

    @pl.when(odd)
    def _():
        row_up[0]()
        row_down[0]()

    @pl.when(jnp.logical_not(odd))
    def _():
        row_down[0]()
        row_up[0]()

    for t in [th_up, th_down] + ph_cells + ph_pack + [th_face, ph_face, row_face]:
        t[0]()
    for t in ph_cells + ph_pack:
        t[1]()
    for t in corner + packs:
        t[0]()
    for t in (th_up, th_down):
        t[1]()
    for t in rowth:
        t[0]()

    def flip(f, value):
        return -value if f in (2, 7) else value

    def own(r):
        return [cells[f, r] for f in range(8)]

    def beside(r):
        if slots == 1:
            return [from_ph[0, f, r] for f in range(8)]
        return [jnp.where(lane < half, from_ph[0, f, r], from_ph[1, f, r]) for f in range(8)]

    def th_low(r):
        x = [cells[f, r, :1] for f in range(8)]
        return [jnp.where(at_north, flip(f, x[f]), from_th[0, f, r]) for f in range(8)]

    def th_high(r):
        x = [cells[f, r, T - 1 :] for f in range(8)]
        return [jnp.where(at_south, flip(f, x[f]), from_th[1, f, r]) for f in range(8)]

    def th_prev(x, ghost):
        return jnp.where(sub == 0, jnp.broadcast_to(ghost, (T, L)), pltpu.roll(x, 1, 0))

    def th_next(x, ghost):
        return jnp.where(sub == T - 1, jnp.broadcast_to(ghost, (T, L)), pltpu.roll(x, T - 1, 0))

    def ph_prev(x, ghost):
        return pltpu.roll(jnp.where(lane == L - 1, ghost, x), 1, 1)

    def ph_next(x, ghost):
        return pltpu.roll(jnp.where(lane == 0, ghost, x), L - 1, 1)

    radial = []
    for r in range(R):
        x = own(r)
        g = beside(r)
        low, high = th_low(r), th_high(r)
        here = derived(x, 2)
        change = face_flux(here, derived([ph_next(a, b) for a, b in zip(x, g)], 2))
        other = face_flux(derived([ph_prev(a, b) for a, b in zip(x, g)], 2), here)
        change = [a - b for a, b in zip(change, other)]
        here = derived(x, 1)
        other = face_flux(here, derived([th_next(a, b) for a, b in zip(x, high)], 1))
        change = [a + b for a, b in zip(change, other)]
        other = face_flux(derived([th_prev(a, b) for a, b in zip(x, low)], 1), here)
        change = [a - b for a, b in zip(change, other)]
        here = derived(x, 0)
        if r:
            other = face_flux(derived(own(r - 1), 0), here)
            change = [a - b for a, b in zip(change, other)]
        if r < R - 1:
            other = face_flux(here, derived(own(r + 1), 0))
            change = [a + b for a, b in zip(change, other)]
        for i in range(5):
            state[i, r] = here[0][i] - step_size * change[i]

    for t in corner + [th_face, ph_face]:
        t[1]()

    def edge_first(r):
        x, g = own(r), beside(r)
        low, high = th_low(r), th_high(r)

        def beside_th(side, edge, at_pole):
            fields = [None, None]
            for f in range(2, 8):
                if slots == 1:
                    far = from_thph[0, side, f - 2, r]
                else:
                    far = jnp.where(
                        lane[:1] < half, from_thph[0, side, f - 2, r], from_thph[1, side, f - 2, r]
                    )
                fields.append(jnp.where(at_pole, flip(f, g[f][edge : edge + 1]), far))
            return fields

        e, eg = emf_first(x), emf_first(g)
        lower = e + th_prev(e, emf_first(low))
        upper = e + th_next(e, emf_first(high))
        lower_g = eg + th_prev(eg, emf_first(beside_th(0, 0, at_north)))
        upper_g = eg + th_next(eg, emf_first(beside_th(1, T - 1, at_south)))
        return (
            0.25 * (lower + ph_prev(lower, lower_g)),
            0.25 * (lower + ph_next(lower, lower_g)),
            0.25 * (upper + ph_prev(upper, upper_g)),
            0.25 * (upper + ph_next(upper, upper_g)),
        )

    def second_parts(r):
        return emf_second(own(r)), emf_second(beside(r))

    def third_parts(r):
        return emf_third(own(r)), emf_third(th_low(r)), emf_third(th_high(r))

    def edge_second(a, b):
        m, mg = a[0] + b[0], a[1] + b[1]
        return 0.25 * (m + ph_prev(m, mg)), 0.25 * (m + ph_next(m, mg))

    def edge_third(a, b):
        h, h_low, h_high = a[0] + b[0], a[1] + b[1], a[2] + b[2]
        return 0.25 * (h + th_prev(h, h_low)), 0.25 * (h + th_next(h, h_high))

    def advance_first(face, two, three):
        return face - step_size * (three[1] - three[0] - (two[1] - two[0]))

    twos, threes, firsts = {}, {}, {}
    for r in range(1, R):
        twos[r] = edge_second(second_parts(r - 1), second_parts(r))
        threes[r] = edge_third(third_parts(r - 1), third_parts(r))
        firsts[r] = advance_first(faces[0, r], twos[r], threes[r])

    def finish(r, ones):
        face = faces[1, r]
        second = face - step_size * (ones[1] - ones[0] - (threes[r + 1][0] - threes[r][0]))
        second_up = th_next(face, face_th[r]) - step_size * (
            ones[3] - ones[2] - (threes[r + 1][1] - threes[r][1])
        )
        second_up = jnp.where(jnp.logical_and(at_south, sub == T - 1), 0.0, second_up)
        face = faces[2, r]
        third = face - step_size * (twos[r + 1][0] - twos[r][0] - (ones[2] - ones[0]))
        third_up = ph_next(face, face_ph[r]) - step_size * (
            twos[r + 1][1] - twos[r][1] - (ones[3] - ones[1])
        )
        faces_new[1, r] = second
        faces_new[2, r] = third
        state[6, r] = 0.5 * (second + second_up)
        state[7, r] = 0.5 * (third + third_up)
        upper = firsts[r + 1]
        if r == R - 1:
            upper = jnp.where(at_top, firsts[r], upper)
        faces_new[0, r] = firsts[r]
        state[5, r] = 0.5 * (firsts[r] + upper)

    for r in range(1, R - 1):
        finish(r, edge_first(r))
    ones_low = edge_first(0)
    ones_high = edge_first(R - 1) if R > 1 else ones_low

    for t in packs + rowth + [row_up, row_down, row_face]:
        t[1]()

    def outer(side, at_end, r):
        x = own(r)
        ghost = [jnp.where(at_end, x[f], from_row[side, f]) for f in range(8)]

        def column(offset, s):
            spread = jnp.broadcast_to(pack_row[s, side], (T, L))
            return jnp.sum(jnp.where(lane == sub + offset, spread, 0.0), axis=1, keepdims=True)

        right_column, left_column = column(0, 0), column(half, slots - 1)
        far = jnp.where(
            lane < half,
            jnp.broadcast_to(right_column, (T, L)),
            jnp.broadcast_to(left_column, (T, L)),
        )
        far = jnp.where(at_end, emf_second(beside(r)), far)

        def th_ghost(which, edge, at_pole, own_ghost):
            fields = [None]
            for f in range(1, 7):
                value = jnp.where(at_end, own_ghost[f], from_rowth[side, which, f - 1])
                fields.append(jnp.where(at_pole, flip(f, ghost[f][edge : edge + 1]), value))
            return emf_third(fields)

        low = th_ghost(0, 0, at_north, th_low(r))
        high = th_ghost(1, T - 1, at_south, th_high(r))
        return ghost, (emf_second(ghost), far), (emf_third(ghost), low, high)

    ghost, two, three = outer(0, at_bottom, 0)
    flux = face_flux(derived(ghost, 0), derived(own(0), 0))
    for i in range(5):
        state[i, 0] = state[i, 0] + step_size * flux[i]
    twos[0] = edge_second(two, second_parts(0))
    threes[0] = edge_third(three, third_parts(0))
    firsts[0] = advance_first(faces[0, 0], twos[0], threes[0])

    ghost, two, three = outer(1, at_top, R - 1)
    flux = face_flux(derived(own(R - 1), 0), derived(ghost, 0))
    for i in range(5):
        state[i, R - 1] = state[i, R - 1] - step_size * flux[i]
    twos[R] = edge_second(second_parts(R - 1), two)
    threes[R] = edge_third(third_parts(R - 1), three)
    firsts[R] = advance_first(face_row[...], twos[R], threes[R])

    finish(0, ones_low)
    if R > 1:
        finish(R - 1, ones_high)

    for t in transfers:
        t[2]()


def on_device(sizes, cells, faces):
    fields, R, T, L = cells.shape
    slots = 1 if sizes[2] == 2 else 2
    f32 = jnp.float32
    copies = 7 + 4 + slots * 6
    return pl.pallas_call(
        functools.partial(kernel, sizes),
        out_shape=(
            jax.ShapeDtypeStruct(cells.shape, f32),
            jax.ShapeDtypeStruct(faces.shape, f32),
        ),
        in_specs=[pl.BlockSpec(memory_space=pl.ANY)] * 2,
        out_specs=[pl.BlockSpec(memory_space=pltpu.VMEM)] * 2,
        scratch_shapes=[
            pltpu.VMEM((fields, R, T, L), f32),
            pltpu.VMEM((3, R, T, L), f32),
            pltpu.VMEM((slots, fields, R, T, L), f32),
            pltpu.VMEM((R, T, L), f32),
            pltpu.VMEM((2, 1, L), f32),
            pltpu.VMEM((slots, 2, 1, L), f32),
            pltpu.VMEM((slots, 2, 1, L), f32),
            pltpu.VMEM((2, fields, R, 1, L), f32),
            pltpu.VMEM((R, 1, L), f32),
            pltpu.VMEM((slots, 2, 6, R, 1, L), f32),
            pltpu.VMEM((2, fields, T, L), f32),
            pltpu.VMEM((T, L), f32),
            pltpu.VMEM((2, 2, 6, 1, L), f32),
            pltpu.SemaphoreType.DMA((2,)),
            pltpu.SemaphoreType.DMA((copies,)),
            pltpu.SemaphoreType.DMA((copies,)),
        ],
        compiler_params=pltpu.CompilerParams(collective_id=0, has_side_effects=True),
    )(cells, faces)


def solution(mesh):
    sizes = (mesh.shape["row"], mesh.shape["th"], mesh.shape["ph"])
    place = P(None, "row", "th", "ph")
    return jax.shard_map(
        functools.partial(on_device, sizes),
        mesh=mesh,
        in_specs=(place, place),
        out_specs=(place, place),
        check_vma=False,
    )
```

time: 30.1 us -> 13.9 us (0.46)
  Pallas kernels: 0 us -> 10.7 us
  starting transfers between devices: 8.47 us -> 0 us
  waiting for transfers between devices: 7.6 us -> 0 us
  other arithmetic: 6.92 us -> 0 us
  local copies, waits for them, and re-layouts: 5.95 us -> 2.35 us
  between operations: 0.97 us -> 0.65 us
    pallas_call x0 -> x1, Pallas kernels: none -> 10.7 us  [on_device(): pl.pallas_call(functools.partial(kernel, sizes), out_shape=(jax.ShapeDtyp...]
    ppermute x6 -> x0, starting transfers between devices: 8.47 us -> none  [the longest x3 5.14 us: padded_2(): lax.ppermute(tail, axis, [(i, (i + 1) % count) for i in range(count)])]
    ppermute x6 -> x0, waiting for transfers between devices: 7.6 us -> none  [the longest x3 5.85 us: padded_2(): lax.ppermute(tail, axis, [(i, (i + 1) % count) for i in range(count)])]
    concatenate x6 -> x0, other arithmetic: 2.32 us -> none  [the longest x2 1.11 us: padded_2(): jnp.concatenate([lax.ppermute(tail, axis, [(i, (i + 1) % count) for i in...]
    sub x7 -> x0, other arithmetic: 1.23 us -> none  [the longest x3 0.86 us: hydro_change(): 0.5 * (flux_cut[tuple(lower_cut)] + flux_cut[tuple(upper_cut)])]
    ppermute x2 -> x0, local copies, waits for them, and re-layouts: 1.04 us -> none  [the longest x1 0.52 us: padded_2(): lax.ppermute(tail, axis, [(i, (i + 1) % count) for i in range(count)])]
    select_n x6 -> x0, other arithmetic: 1.01 us -> none  [the longest x1 0.37 us: fix_radial(): highest = jnp.where(at_top, padded[:, -2:-1], padded[:, -1:])]
    concatenate x1 -> x0, local copies, waits for them, and re-layouts: 0.9 us -> none  [on_device(): source = jnp.concatenate([cells, faces], axis=0)]
  transfers between devices with their start and end apart: 6 -> 0, of which waited for: 4 -> 0; matrix products, arithmetic and copies ran while one was open for 2% -> 0% of each run, Pallas kernels for 0% -> 0%
where the time goes in v1:
time: 13.9 us; the launch traced here: 13.7 us
  Pallas kernels  10.7 us (77%)
  local copies, waits for them, and re-layouts  2.35 us (17%)
  between operations  0.65 us (5%)
    pallas_call x1, Pallas kernels, on_device(): pl.pallas_call(functools.partial(kernel, sizes), out_shape=(jax.ShapeDtyp...  10.7 us
    unnamed x4, local copies, waits for them, and re-layouts  2.35 us

profile of v1, /device:TPU:0, one launch (start us, length us, event | category | flops | bytes accessed | tf_op | source)
XLA Modules:
  0.0 13.7 jit_solution(14371686930711598968)
XLA Ops:
  0.6 10.7 %shard_map.41 = (f32[8,4,16,128]{3,2,1,0:T(8,128)}, f32[3,4,16,128]{3,2,1,0:T(8,128)}) custom-call(f32[8,4,16,128]{3,2,1,0:T(8,128)} %cells_hbm.1, f32[3,4,16,128]{3,2,1,0:T(8,128)} %faces_hbm.1), custom_call_target="tpu_custom_call" | custom-call | tf_op jit(solution)/shard_map/pallas_call | solution.py:431
  11.4 0.0 copy-start
  11.4 1.7 %copy.6 = f32[8,4,16,128]{3,2,1,0:T(8,128)} copy(f32[8,4,16,128]{3,2,1,0:T(8,128)} %get-tuple-element.4) | data formatting | bytes 524288
  13.1 0.0 copy-done
  13.1 0.6 %copy.7 = f32[3,4,16,128]{3,2,1,0:T(8,128)} copy(f32[3,4,16,128]{3,2,1,0:T(8,128)S(1)} %copy-done) | data formatting | bytes 196608
Async XLA Ops:
  11.4 1.7 %copy-start = (f32[3,4,16,128]{3,2,1,0:T(8,128)S(1)}, f32[3,4,16,128]{3,2,1,0:T(8,128)}, u32[]{:S(2)}) copy-start(f32[3,4,16,128]{3,2,1,0:T(8,128)} %get-tuple-element.5) | copy-start | bytes 294916

commit v2 on v1

--- a/solution.py
+++ b/solution.py
@@ -423,17 +423,26 @@
         t[2]()
 
 
+def store(state, faces_new, state_hbm, faces_hbm, sem):
+    copies = [
+        pltpu.make_async_copy(state, state_hbm, sem.at[0]),
+        pltpu.make_async_copy(faces_new, faces_hbm, sem.at[1]),
+    ]
+    for copy in copies:
+        copy.start()
+    for copy in copies:
+        copy.wait()
+
+
 def on_device(sizes, cells, faces):
     fields, R, T, L = cells.shape
     slots = 1 if sizes[2] == 2 else 2
     f32 = jnp.float32
     copies = 7 + 4 + slots * 6
-    return pl.pallas_call(
+    whole = (jax.ShapeDtypeStruct(cells.shape, f32), jax.ShapeDtypeStruct(faces.shape, f32))
+    results = pl.pallas_call(
         functools.partial(kernel, sizes),
-        out_shape=(
-            jax.ShapeDtypeStruct(cells.shape, f32),
-            jax.ShapeDtypeStruct(faces.shape, f32),
-        ),
+        out_shape=(pltpu.VMEM(cells.shape, f32), pltpu.VMEM(faces.shape, f32)),
         in_specs=[pl.BlockSpec(memory_space=pl.ANY)] * 2,
         out_specs=[pl.BlockSpec(memory_space=pltpu.VMEM)] * 2,
         scratch_shapes=[
@@ -456,6 +465,13 @@
         ],
         compiler_params=pltpu.CompilerParams(collective_id=0, has_side_effects=True),
     )(cells, faces)
+    return pl.pallas_call(
+        store,
+        out_shape=whole,
+        in_specs=[pl.BlockSpec(memory_space=pltpu.VMEM)] * 2,
+        out_specs=[pl.BlockSpec(memory_space=pl.ANY)] * 2,
+        scratch_shapes=[pltpu.SemaphoreType.DMA((2,))],
+    )(*[pltpu.with_memory_space_constraint(x, pltpu.VMEM) for x in results])
 
 
 def solution(mesh):

time: 13.9 us -> 11.5 us (0.83)
  local copies, waits for them, and re-layouts: 2.35 us -> 0 us
    unnamed x4 -> x0, local copies, waits for them, and re-layouts: 2.35 us -> none
    pallas_call x1 -> x2, Pallas kernels: 10.7 us -> 10.7 us  [the longest x1 10 us: on_device(): pl.pallas_call(functools.partial(kernel, sizes), out_shape=(pltpu.VMEM(ce...]
where the time goes in v2:
time: 11.5 us; the launch traced here: 11.4 us
  Pallas kernels  10.7 us (93%)
  between operations  0.64 us (6%)
    pallas_call x1, Pallas kernels, on_device(): pl.pallas_call(functools.partial(kernel, sizes), out_shape=(pltpu.VMEM(ce...  10 us
    pallas_call x1, Pallas kernels, on_device(): pl.pallas_call(store, out_shape=whole, in_specs=[pl.BlockSpec(memory_spac...  0.75 us

profile of v2, /device:TPU:0, one launch (start us, length us, event | category | flops | bytes accessed | tf_op | source)
XLA Modules:
  0.0 11.4 jit_solution(9883439363580254853)
XLA Ops:
  0.6 10.0 %shard_map.41 = (f32[8,4,16,128]{3,2,1,0:T(8,128)S(1)}, f32[3,4,16,128]{3,2,1,0:T(8,128)S(1)}) custom-call(f32[8,4,16,128]{3,2,1,0:T(8,128)} %cells_hbm.1, f32[3,4,16,128]{3,2,1,0:T(8,128)} %faces_hbm.1), custom_call_target="tpu_custom_call" | custom-call | tf_op jit(solution)/shard_map/pallas_call | solution.py:443
  10.6 0.7 %shard_map.42 = (f32[8,4,16,128]{3,2,1,0:T(8,128)}, f32[3,4,16,128]{3,2,1,0:T(8,128)}) custom-call(f32[8,4,16,128]{3,2,1,0:T(8,128)S(1)} %get-tuple-element.4.state, f32[3,4,16,128]{3,2,1,0:T(8,128)S(1)} %get-tuple-element.5.faces_new), custom_call_target="tpu_custom_call" | custom-call | tf_op jit(solution)/shard_map/pallas_call | solution.py:468

commit v3 on v2

--- a/solution.py
+++ b/solution.py
@@ -68,7 +68,6 @@
     from_ph,
     face_ph,
     pack_own,
-    pack_ph,
     pack_row,
     from_th,
     face_th,
@@ -93,19 +92,32 @@
     ph_targets = [{"ph": left}] if n_ph == 2 else [{"ph": left}, {"ph": right}]
     slots = len(ph_targets)
 
+    odd = lax.rem(row, 2) == 1
+    even = jnp.logical_not(odd)
+    both = jnp.logical_and
+    not_bottom, not_top = jnp.logical_not(at_bottom), jnp.logical_not(at_top)
+    not_north, not_south = jnp.logical_not(at_north), jnp.logical_not(at_south)
+    pair_up, pair_down = not_top, not_bottom
+
     barrier = pltpu.get_barrier_semaphore()
-    greet = [
-        (jnp.logical_not(at_bottom), below),
-        (jnp.logical_not(at_top), above),
-        (jnp.logical_not(at_north), north),
-        (jnp.logical_not(at_south), south),
-    ]
+    sides = [(not_bottom, below), (not_top, above), (not_north, north), (not_south, south)]
+    greet = list(sides)
+    for who in ph_targets:
+        greet.append((None, who))
+        greet.extend((exists, {**side, **who}) for exists, side in sides)
+    for pair, radial in ((pair_down, below), (pair_up, above)):
+        for exists, polar in sides[2:]:
+            greet.append((both(pair, exists), {**radial, **polar}))
+    peers = slots
     for exists, who in greet:
-        @pl.when(exists)
-        def _():
+        if exists is None:
             pl.semaphore_signal(barrier, inc=1, device_id=who, device_id_type=MESH)
-    for who in ph_targets:
-        pl.semaphore_signal(barrier, inc=1, device_id=who, device_id_type=MESH)
+        else:
+            peers = peers + exists.astype(jnp.int32)
+
+            @pl.when(exists)
+            def _():
+                pl.semaphore_signal(barrier, inc=1, device_id=who, device_id_type=MESH)
 
     load_cells = pltpu.make_async_copy(cells_hbm, cells, local_sem.at[0])
     load_faces = pltpu.make_async_copy(faces_hbm, faces, local_sem.at[1])
@@ -141,7 +153,6 @@
         transfers.append(entry)
         return entry
 
-    not_bottom, not_top, not_north, not_south = [g[0] for g in greet]
     first_row, last_row = pl.ds(0, 1), pl.ds(T - 1, 1)
     row_up = transfer(cells.at[:, R - 1], from_row.at[0], above, not_top, not_bottom)
     row_down = transfer(cells.at[:, 0], from_row.at[1], below, not_bottom, not_top)
@@ -150,48 +161,42 @@
     th_down = transfer(cells.at[:, :, first_row], from_th.at[1], north, not_north, not_south)
     th_face = transfer(faces.at[1, :, first_row], face_th, north, not_north, not_south)
     ph_cells = [transfer(cells, from_ph.at[s], ph_targets[s]) for s in range(slots)]
-    ph_pack = [transfer(pack_own, pack_ph.at[s], ph_targets[s]) for s in range(slots)]
     ph_face = transfer(faces.at[2], face_ph, ph_targets[0])
-    corner = []
+    corner, packs = [], []
     for s in range(slots):
-        corner.append(
-            transfer(
-                from_ph.at[s, pl.ds(2, 6), :, last_row], from_thph.at[s, 0], south, not_south, not_north
+        who = ph_targets[s]
+        for side, strip, towards, sends, receives in (
+            (0, last_row, south, not_south, not_north),
+            (1, first_row, north, not_north, not_south),
+        ):
+            src = cells.at[pl.ds(2, 6), :, strip]
+            corner.append(
+                transfer(src, from_thph.at[s, side], {**towards, **who}, sends, receives)
             )
-        )
-        corner.append(
-            transfer(
-                from_ph.at[s, pl.ds(2, 6), :, first_row], from_thph.at[s, 1], north, not_north, not_south
+        for side, towards, sends, receives in (
+            (0, above, not_top, not_bottom),
+            (1, below, not_bottom, not_top),
+        ):
+            src = pack_own.at[1 - side]
+            packs.append(transfer(src, pack_row.at[s, side], {**towards, **who}, sends, receives))
+    direct = []
+    for side, layer, radial, sends_row, gets_row in (
+        (0, R - 1, above, pair_up, pair_down),
+        (1, 0, below, pair_down, pair_up),
+    ):
+        for where, strip, polar, sends_th, gets_th in (
+            (0, last_row, south, not_south, not_north),
+            (1, first_row, north, not_north, not_south),
+        ):
+            direct.append(
+                transfer(
+                    cells.at[pl.ds(1, 6), layer, strip],
+                    from_rowth.at[side, where],
+                    {**radial, **polar},
+                    both(sends_row, sends_th),
+                    both(gets_row, gets_th),
+                )
             )
-        )
-    packs = []
-    for s in range(slots):
-        packs.append(
-            transfer(pack_ph.at[s, 1], pack_row.at[s, 0], above, not_top, not_bottom)
-        )
-        packs.append(
-            transfer(pack_ph.at[s, 0], pack_row.at[s, 1], below, not_bottom, not_top)
-        )
-    rowth = []
-    for side, has in ((0, not_north), (1, not_south)):
-        rowth.append(
-            transfer(
-                from_th.at[side, pl.ds(1, 6), R - 1],
-                from_rowth.at[0, side],
-                above,
-                jnp.logical_and(not_top, has),
-                jnp.logical_and(not_bottom, has),
-            )
-        )
-        rowth.append(
-            transfer(
-                from_th.at[side, pl.ds(1, 6), 0],
-                from_rowth.at[1, side],
-                below,
-                jnp.logical_and(not_bottom, has),
-                jnp.logical_and(not_top, has),
-            )
-        )
 
     lane = lax.broadcasted_iota(jnp.int32, (T, L), 1)
     sub = lax.broadcasted_iota(jnp.int32, (T, L), 0)
@@ -207,31 +212,24 @@
         pack_own[where] = jnp.sum(spread, axis=0, keepdims=True)
     load_faces.wait()
 
-    peers = slots + sum(exists.astype(jnp.int32) for exists, _ in greet)
     pl.semaphore_wait(barrier, peers)
-
-    odd = lax.rem(row, 2) == 1
+    for t in ph_cells + direct + corner + [th_up, th_down] + packs:
+        t[0]()
 
     @pl.when(odd)
     def _():
-        row_up[0]()
-        row_down[0]()
-
-    @pl.when(jnp.logical_not(odd))
+        for t in (row_down, row_face, row_up):
+            t[0]()
+
+    @pl.when(even)
     def _():
-        row_down[0]()
-        row_up[0]()
-
-    for t in [th_up, th_down] + ph_cells + ph_pack + [th_face, ph_face, row_face]:
+        for t in (row_up, row_down, row_face):
+            t[0]()
+
+    for t in (th_face, ph_face):
         t[0]()
-    for t in ph_cells + ph_pack:
+    for t in ph_cells + [th_up, th_down]:
         t[1]()
-    for t in corner + packs:
-        t[0]()
-    for t in (th_up, th_down):
-        t[1]()
-    for t in rowth:
-        t[0]()
 
     def flip(f, value):
         return -value if f in (2, 7) else value
@@ -369,7 +367,7 @@
     ones_low = edge_first(0)
     ones_high = edge_first(R - 1) if R > 1 else ones_low
 
-    for t in packs + rowth + [row_up, row_down, row_face]:
+    for t in packs + direct + [row_up, row_down, row_face]:
         t[1]()
 
     def outer(side, at_end, r):
@@ -438,7 +436,7 @@
     fields, R, T, L = cells.shape
     slots = 1 if sizes[2] == 2 else 2
     f32 = jnp.float32
-    copies = 7 + 4 + slots * 6
+    copies = 11 + slots * 5
     whole = (jax.ShapeDtypeStruct(cells.shape, f32), jax.ShapeDtypeStruct(faces.shape, f32))
     results = pl.pallas_call(
         functools.partial(kernel, sizes),
@@ -451,7 +449,6 @@
             pltpu.VMEM((slots, fields, R, T, L), f32),
             pltpu.VMEM((R, T, L), f32),
             pltpu.VMEM((2, 1, L), f32),
-            pltpu.VMEM((slots, 2, 1, L), f32),
             pltpu.VMEM((slots, 2, 1, L), f32),
             pltpu.VMEM((2, fields, R, 1, L), f32),
             pltpu.VMEM((R, 1, L), f32),

time: 11.5 us -> 10.4 us (0.904)
  Pallas kernels: 10.7 us -> 9.67 us
    pallas_call x1, Pallas kernels: 10 us -> 8.92 us  [on_device(): pl.pallas_call(functools.partial(kernel, sizes), out_shape=(pltpu.VMEM(ce...]
where the time goes in v3:
time: 10.4 us; the launch traced here: 10.3 us
  Pallas kernels  9.67 us (93%)
  between operations  0.64 us (6%)
    pallas_call x1, Pallas kernels, on_device(): pl.pallas_call(functools.partial(kernel, sizes), out_shape=(pltpu.VMEM(ce...  8.92 us
    pallas_call x1, Pallas kernels, on_device(): pl.pallas_call(store, out_shape=whole, in_specs=[pl.BlockSpec(memory_spac...  0.75 us

profile of v3, /device:TPU:0, one launch (start us, length us, event | category | flops | bytes accessed | tf_op | source)
XLA Modules:
  0.0 10.3 jit_solution(6016875164747985568)
XLA Ops:
  0.6 8.9 %shard_map.41 = (f32[8,4,16,128]{3,2,1,0:T(8,128)S(1)}, f32[3,4,16,128]{3,2,1,0:T(8,128)S(1)}) custom-call(f32[8,4,16,128]{3,2,1,0:T(8,128)} %cells_hbm.1, f32[3,4,16,128]{3,2,1,0:T(8,128)} %faces_hbm.1), custom_call_target="tpu_custom_call" | custom-call | tf_op jit(solution)/shard_map/pallas_call | solution.py:441
  9.6 0.7 %shard_map.42 = (f32[8,4,16,128]{3,2,1,0:T(8,128)}, f32[3,4,16,128]{3,2,1,0:T(8,128)}) custom-call(f32[8,4,16,128]{3,2,1,0:T(8,128)S(1)} %get-tuple-element.4.state, f32[3,4,16,128]{3,2,1,0:T(8,128)S(1)} %get-tuple-element.5.faces_new), custom_call_target="tpu_custom_call" | custom-call | tf_op jit(solution)/shard_map/pallas_call | solution.py:465

commit v4 on v3

--- a/solution.py
+++ b/solution.py
@@ -218,18 +218,26 @@
 
     @pl.when(odd)
     def _():
-        for t in (row_down, row_face, row_up):
+        for t in (row_down, row_face):
             t[0]()
 
     @pl.when(even)
     def _():
-        for t in (row_up, row_down, row_face):
-            t[0]()
+        row_up[0]()
 
     for t in (th_face, ph_face):
         t[0]()
-    for t in ph_cells + [th_up, th_down]:
+    for t in ph_cells:
         t[1]()
+
+    @pl.when(odd)
+    def _():
+        row_up[0]()
+
+    @pl.when(even)
+    def _():
+        for t in (row_down, row_face):
+            t[0]()
 
     def flip(f, value):
         return -value if f in (2, 7) else value
@@ -262,19 +270,11 @@
     def ph_next(x, ghost):
         return pltpu.roll(jnp.where(lane == 0, ghost, x), L - 1, 1)
 
-    radial = []
     for r in range(R):
-        x = own(r)
-        g = beside(r)
-        low, high = th_low(r), th_high(r)
+        x, g = own(r), beside(r)
         here = derived(x, 2)
         change = face_flux(here, derived([ph_next(a, b) for a, b in zip(x, g)], 2))
         other = face_flux(derived([ph_prev(a, b) for a, b in zip(x, g)], 2), here)
-        change = [a - b for a, b in zip(change, other)]
-        here = derived(x, 1)
-        other = face_flux(here, derived([th_next(a, b) for a, b in zip(x, high)], 1))
-        change = [a + b for a, b in zip(change, other)]
-        other = face_flux(derived([th_prev(a, b) for a, b in zip(x, low)], 1), here)
         change = [a - b for a, b in zip(change, other)]
         here = derived(x, 0)
         if r:
@@ -285,6 +285,16 @@
             change = [a + b for a, b in zip(change, other)]
         for i in range(5):
             state[i, r] = here[0][i] - step_size * change[i]
+
+    for t in (th_up, th_down):
+        t[1]()
+    for r in range(R):
+        x, low, high = own(r), th_low(r), th_high(r)
+        here = derived(x, 1)
+        change = face_flux(here, derived([th_next(a, b) for a, b in zip(x, high)], 1))
+        other = face_flux(derived([th_prev(a, b) for a, b in zip(x, low)], 1), here)
+        for i in range(5):
+            state[i, r] = state[i, r] - step_size * (change[i] - other[i])
 
     for t in corner + [th_face, ph_face]:
         t[1]()

time: 10.4 us -> 10.3 us (level)
  Pallas kernels: 9.67 us -> 9.55 us
    pallas_call x1, Pallas kernels: 8.92 us -> 8.8 us  [on_device(): pl.pallas_call(functools.partial(kernel, sizes), out_shape=(pltpu.VMEM(ce...]
where the time goes in v4:
time: 10.3 us; the launch traced here: 10.2 us
  Pallas kernels  9.55 us (93%)
  between operations  0.64 us (6%)
    pallas_call x1, Pallas kernels, on_device(): pl.pallas_call(functools.partial(kernel, sizes), out_shape=(pltpu.VMEM(ce...  8.8 us
    pallas_call x1, Pallas kernels, on_device(): pl.pallas_call(store, out_shape=whole, in_specs=[pl.BlockSpec(memory_spac...  0.75 us

profile of v4, /device:TPU:0, one launch (start us, length us, event | category | flops | bytes accessed | tf_op | source)
XLA Modules:
  0.0 10.2 jit_solution(6951797745839323131)
XLA Ops:
  0.6 8.8 %shard_map.41 = (f32[8,4,16,128]{3,2,1,0:T(8,128)S(1)}, f32[3,4,16,128]{3,2,1,0:T(8,128)S(1)}) custom-call(f32[8,4,16,128]{3,2,1,0:T(8,128)} %cells_hbm.1, f32[3,4,16,128]{3,2,1,0:T(8,128)} %faces_hbm.1), custom_call_target="tpu_custom_call" | custom-call | tf_op jit(solution)/shard_map/pallas_call | solution.py:451
  9.4 0.7 %shard_map.42 = (f32[8,4,16,128]{3,2,1,0:T(8,128)}, f32[3,4,16,128]{3,2,1,0:T(8,128)}) custom-call(f32[8,4,16,128]{3,2,1,0:T(8,128)S(1)} %get-tuple-element.4.state, f32[3,4,16,128]{3,2,1,0:T(8,128)S(1)} %get-tuple-element.5.faces_new), custom_call_target="tpu_custom_call" | custom-call | tf_op jit(solution)/shard_map/pallas_call | solution.py:475
